TPU v7x, 128 devices: a whole 4x4x4 slice. The times are simulated.
128 devices in a mesh: section: 32 (over y, z, core), tensor: 4 (over x).
Axes of the slice: x: 4, y: 4, z: 4, core: 2. Of those that a mesh axis runs over, the one named last changes fastest.
Arguments:
- section_input: bfloat16 [32, 512, 4096], P('section', 'tensor'), may hold values from -6 to 6
- history: bfloat16 [32, 7, 512, 4096], P('section', None, 'tensor'), may hold values from -6 to 6
- query_weight: bfloat16 [32, 4096, 3072], P('section', None, 'tensor'), may hold values from -0.4 to 0.4
- key_weight: bfloat16 [32, 4096, 512], P('section', None, 'tensor'), may hold values from -0.4 to 0.4
- value_weight: bfloat16 [32, 4096, 512], P('section', None, 'tensor'), may hold values from -0.09375 to 0.09375
- output_weight: bfloat16 [32, 3072, 4096], P('section', 'tensor'), may hold values from -0.5 to 0.5
- mix_weights: float32 [32, 8], replicated, may hold values from 0.2 to 0.6
Outputs:
- next_input: bfloat16 [32, 512, 4096], P('section', 'tensor')
All inputs are finite; a program needn't handle non-finite values.
Results may differ from a plain program's by a relative error of at most 0.013.
The roundings to bfloat16 on the way count: a program that leaves them out, or rounds other values in their place, can miss the bound.
Values may be sent and summed in bfloat16 or wider, within the bound.
No kernel may reach another device: no remote copies, remote signals or barrier semaphores. Data moves between devices by JAX's collectives and lax.ppermute only.
A program may use at most 128 MiB of HBM per device.

v0:
```python
import math
import jax
import jax.numpy as jnp
from jax import lax
from jax.sharding import PartitionSpec as P

HEAD_DIM = 64
DILATION_STRIDE = 4


def passed_along(value, axis, steps):
    count = lax.axis_size(axis)
    first, last = (max(0, -steps), min(count, count - steps))
    return lax.ppermute(value, axis, [(source, source + steps) for source in range(first, last)])


def from_behind(block, axis, distance):
    devices = range(lax.axis_size(axis))
    route = [((i - distance) % len(devices), i) for i in devices]
    return lax.ppermute(block, axis, route)


def normalize(token_rows):
    values = token_rows.astype(jnp.float32)
    inv_scale = lax.rsqrt(jnp.mean(values * values, axis=-1, keepdims=True) + 1e-05)
    return (values * inv_scale).astype(jnp.bfloat16)


def table_row(table, wanted):
    one_hot = (jnp.arange(table.shape[0], dtype=jnp.int32) == wanted).astype(jnp.float32)
    return jnp.sum(one_hot[:, None] * table, axis=0)


def attend(query_rows, key_rows, value_rows, first_row):
    scores = jnp.einsum(
        "tgjd,sgd->gjts", query_rows, key_rows, preferred_element_type=jnp.float32
    ) / math.sqrt(HEAD_DIM)
    row_positions = first_row + jnp.arange(query_rows.shape[0], dtype=jnp.int32)
    key_positions = jnp.arange(key_rows.shape[0], dtype=jnp.int32)
    scores = jnp.where(row_positions[:, None] >= key_positions[None, :], scores, -1e30)
    softmax_weights = jax.nn.softmax(scores, axis=-1).astype(jnp.bfloat16)
    heads_out = jnp.einsum(
        "gjts,sgd->tgjd", softmax_weights, value_rows, preferred_element_type=jnp.float32
    )
    return heads_out.astype(jnp.bfloat16)


def on_device(
    section_input, history, query_weight, key_weight, value_weight, output_weight, mix_weights
):
    token_rows = section_input[0]
    current_section = lax.axis_index("section")
    slots = history.shape[1]
    self_coefficient = table_row(mix_weights, current_section)
    history_sum = jnp.zeros(token_rows.shape, jnp.float32)
    for history_slot in range(1, slots + 1):
        received_block = passed_along(
            history[0, history_slot - 1], "section", DILATION_STRIDE * history_slot
        )
        factor = jnp.where(
            current_section >= DILATION_STRIDE * history_slot,
            self_coefficient[history_slot],
            jnp.float32(0.0),
        )
        history_sum = history_sum + factor * received_block.astype(jnp.float32)
    normed = normalize(token_rows)
    query_local = query_weight[0]
    key_local = key_weight[0]
    value_local = value_weight[0]
    row_piece = lax.all_gather(normed, "tensor", axis=0, tiled=True)
    query_part = jnp.dot(row_piece, query_local, preferred_element_type=jnp.float32).astype(
        jnp.bfloat16
    )
    key_part = jnp.dot(row_piece, key_local, preferred_element_type=jnp.float32).astype(
        jnp.bfloat16
    )
    value_part = jnp.dot(row_piece, value_local, preferred_element_type=jnp.float32).astype(
        jnp.bfloat16
    )
    projected = jnp.concatenate([query_part, key_part, value_part], axis=1)
    query_width = query_local.shape[1]
    kv_width = key_local.shape[1]
    seq_len = projected.shape[0]
    groups = kv_width // HEAD_DIM
    per_group = query_width // kv_width
    query_rows = projected[:, :query_width].reshape(seq_len, groups, per_group, HEAD_DIM)
    key_rows = projected[:, query_width : query_width + kv_width].reshape(seq_len, groups, HEAD_DIM)
    value_rows = projected[:, query_width + kv_width :].reshape(seq_len, groups, HEAD_DIM)
    block_rows = 512
    block_count = seq_len // block_rows
    blocked = query_rows.reshape(block_count, block_rows, groups, per_group, HEAD_DIM)
    starts = jnp.arange(block_count, dtype=jnp.int32) * block_rows
    attended = lax.map(
        lambda paired: attend(paired[0], key_rows, value_rows, paired[1]), (blocked, starts)
    )
    heads_out = attended.reshape(seq_len, query_width)
    output_local = output_weight[0]
    row_piece = heads_out
    partial_term = jnp.dot(row_piece, output_local, preferred_element_type=jnp.float32).astype(
        jnp.bfloat16
    )
    attention_sum = lax.psum_scatter(
        lax.optimization_barrier(partial_term).astype(jnp.float32).astype(jnp.bfloat16),
        "tensor",
        scatter_dimension=0,
        tiled=True,
    ).astype(jnp.float32)
    block_out = (token_rows.astype(jnp.float32) + attention_sum).astype(jnp.bfloat16)
    mixed = (self_coefficient[0] * block_out.astype(jnp.float32) + history_sum).astype(jnp.bfloat16)
    forwarded = from_behind(mixed, "section", 1)
    return forwarded[None]


def solution(mesh):
    placed = (
        P("section", "tensor", None),
        P("section", None, "tensor", None),
        P("section", None, "tensor"),
        P("section", None, "tensor"),
        P("section", None, "tensor"),
        P("section", "tensor", None),
        P(),
    )
    return jax.shard_map(
        on_device,
        mesh=mesh,
        in_specs=placed,
        out_specs=P("section", "tensor", None),
        check_vma=False,
    )
```

profile of v0, /device:TPU:0, one launch (start us, length us, event | category | flops | bytes accessed | tf_op | source)
XLA Modules:
  0.0 245.2 jit_solution(5167761586907813160)
XLA Ops:
  6.5 1.6 fusion.13
  8.2 2.5 %fusion.14 = bf16[128,4096]{1,0:T(8,128)(2,1)} fusion(bf16[1,128,4096]{2,1,0:T(8,128)(2,1)} %param.7, f32[128]{0:T(128)S(1)} %add_rsqrt_fusion), kind=kLoop, calls=%fused_computation.18 | loop fusion | flops 1572864 | bytes 2097664 | tf_op jit(solution)/shard_map/convert_element_type | solution.py:26
  10.8 50.7 %all-gather.2.cloned.1.call-done = bf16[512,4096]{1,0:T(8,128)(2,1)} async-done(((bf16[128,4096]{1,0:T(8,128)(2,1)}), bf16[512,4096]{1,0:T(8,128)(2,1)}) %all-gather.2.cloned.1.call-update) | async-done | bytes 4194320 | tf_op jit(solution)/shard_map/all_gather | solution.py:70
  61.5 7.5 %fusion.19 = bf16[512,768]{1,0:T(8,128)(2,1)S(1)} fusion(bf16[512,4096]{1,0:T(8,128)(2,1)} %all-gather.2.cloned.1.call-done, bf16[1,4096,768]{2,1,0:T(8,128)(2,1)} %param.9), kind=kOutput, calls=%fused_computation.23 | convolution fusion | flops 3221618688 | bytes 11272192 | tf_op jit(solution)/shard_map/dot_general | solution.py:71
  69.2 3.7 %convolution_convert_fusion = bf16[512,128]{0,1:T(8,128)(2,1)S(1)} fusion(bf16[512,4096]{1,0:T(8,128)(2,1)} %all-gather.2.cloned.1.call-done, bf16[1,4096,128]{2,1,0:T(8,128)(2,1)S(1)} %copy-done), kind=kOutput, calls=%fused_computation.24 | convolution fusion | flops 536936448 | bytes 5373952 | tf_op jit(solution)/shard_map/dot_general | solution.py:74
  72.9 7.3 %fusion.27 = (f32[2,6,512]{2,1,0:T(8,128)S(1)}, f32[2,6,512,512]{2,3,1,0:T(8,128)}) fusion(pred[512,512]{0,1:T(8,128)(4,1)S(1)} %iota_compare_fusion, bf16[512,2,64,1]{0,2,3,1:T(8,128)(2,1)S(1)} %bitcast.80, bf16[512,2,6,64]{0,3,2,1:T(8,128)(2,1)S(1)} %bitcast.79), kind=kOutput, calls=%fused_computation.42 | convolution fusion | flops 415236608 | bytes 13787136 | tf_op jit(solution)/shard_map/while/body/eval_jaxpr/sub | solution.py:41
  80.2 3.8 %convolution_convert_fusion.1 = bf16[512,128]{0,1:T(8,128)(2,1)S(1)} fusion(bf16[512,4096]{1,0:T(8,128)(2,1)} %all-gather.2.cloned.1.call-done, bf16[1,4096,128]{2,1,0:T(8,128)(2,1)S(1)} %copy-done.2), kind=kOutput, calls=%fused_computation.25 | convolution fusion | flops 536936448 | bytes 5373952 | tf_op jit(solution)/shard_map/dot_general | solution.py:77
  84.1 6.0 %fusion.18 = bf16[2,64,6,512]{3,1,2,0:T(8,128)(2,1)S(1)} fusion(bf16[512,2,64,1]{0,2,3,1:T(8,128)(2,1)S(1)} %bitcast.81, f32[2,6,512,512]{2,3,1,0:T(8,128)} %get-tuple-element.36, f32[2,6,512]{2,1,0:T(8,128)S(1)} %get-tuple-element.35), kind=kOutput, calls=%fused_computation.22 | convolution fusion | flops 409337856 | bytes 13524992 | tf_op jit(solution)/shard_map/while/body/eval_jaxpr/gjts,sgd->tgjd/dot_general | solution.py:42
  90.1 5.2 %fusion.10 = bf16[512,4096]{1,0:T(8,128)(2,1)} fusion(bf16[512,768]{0,1:T(8,128)(2,1)S(1)} %bitcast.84, bf16[1,768,4096]{2,1,0:T(8,128)(2,1)S(1)} %bitcast.83), kind=kOutput, calls=%fused_computation.13 | convolution fusion | flops 3223322624 | bytes 11272192 | tf_op jit(solution)/shard_map/dot_general | solution.py:99
  95.4 5.6 %slice_bitcast_fusion.6 = (bf16[128,4096]{1,0:T(8,128)(2,1)S(1)}, bf16[128,4096]{1,0:T(8,128)(2,1)}, bf16[128,4096]{1,0:T(8,128)(2,1)}, bf16[128,4096]{1,0:T(8,1...) fusion(bf16[1,7,128,4096]{3,2,1,0:T(8,128)(2,1)} %param.8), kind=kLoop, calls=%fused_computation.34 | loop fusion | bytes 14680064 | tf_op jit(solution)/shard_map/squeeze | solution.py:58
  100.9 5.1 %collective-permute-start = (bf16[128,4096]{1,0:T(8,128)(2,1)S(1)}, bf16[128,4096]{1,0:T(8,128)(2,1)S(1)}, u32[]{:S(2)}, u32[]{:S(2)}) collective-permute-start(bf16[128,4096]{1,0:T(8,128)(2,1)S(1)} %get-tuple-element.13), channel_id=1, source_target_pairs={{0,16},{4,20},{8,24},{12,28},{16,32},{20,36},{24,40},{28,44},{32,4... | collective-permute-start | bytes 3145736 | tf_op jit(solution)/shard_map/ppermute | solution.py:14
  106.1 3.4 %collective-permute-start.1 = (bf16[128,4096]{1,0:T(8,128)(2,1)S(1)}, bf16[128,4096]{1,0:T(8,128)(2,1)S(1)}, u32[]{:S(2)}, u32[]{:S(2)}) collective-permute-start(bf16[128,4096]{1,0:T(8,128)(2,1)S(1)} %get-tuple-element.24), channel_id=1, source_target_pairs={{0,32},{4,36},{8,40},{12,44},{16,48},{20,52},{24,56},{28,60},{32,6... | collective-permute-start | bytes 3145736 | tf_op jit(solution)/shard_map/ppermute | solution.py:14
  109.5 4.7 %collective-permute-start.2 = (bf16[128,4096]{1,0:T(8,128)(2,1)}, bf16[128,4096]{1,0:T(8,128)(2,1)}, u32[]{:S(2)}, u32[]{:S(2)}) collective-permute-start(bf16[128,4096]{1,0:T(8,128)(2,1)} %get-tuple-element.22), channel_id=1, source_target_pairs={{0,48},{4,52},{8,56},{12,60},{16,64},{20,68},{24,72},{28,76},{32,8... | collective-permute-start | bytes 3145736 | tf_op jit(solution)/shard_map/ppermute | solution.py:14
  114.2 2.8 %collective-permute-start.3 = (bf16[128,4096]{1,0:T(8,128)(2,1)}, bf16[128,4096]{1,0:T(8,128)(2,1)}, u32[]{:S(2)}, u32[]{:S(2)}) collective-permute-start(bf16[128,4096]{1,0:T(8,128)(2,1)} %get-tuple-element.20), channel_id=1, source_target_pairs={{0,64},{4,68},{8,72},{12,76},{16,80},{20,84},{24,88},{28,92},{32,9... | collective-permute-start | bytes 3145736 | tf_op jit(solution)/shard_map/ppermute | solution.py:14
  117.0 2.3 collective-permute-start.4
  119.3 8.9 %collective-permute-done = bf16[128,4096]{1,0:T(8,128)(2,1)S(1)} collective-permute-done((bf16[128,4096]{1,0:T(8,128)(2,1)S(1)}, bf16[128,4096]{1,0:T(8,128)(2,1)S(1)}, u32[]{:S(2)}, u32[]{:S(2)}) %collective-permute-start) | collective-permute-done | bytes 1048608 | tf_op jit(solution)/shard_map/ppermute | solution.py:14
  128.2 29.9 %collective-permute-start.5 = (bf16[128,4096]{1,0:T(8,128)(2,1)}, bf16[128,4096]{1,0:T(8,128)(2,1)}, u32[]{:S(2)}, u32[]{:S(2)}) collective-permute-start(bf16[128,4096]{1,0:T(8,128)(2,1)} %get-tuple-element.26), channel_id=1, source_target_pairs={{0,96},{4,100},{8,104},{12,108},{16,112},{20,116},{24,120},{28,124... | collective-permute-start | bytes 3145736 | tf_op jit(solution)/shard_map/ppermute | solution.py:14
  158.2 20.5 %collective-permute-start.6 = (bf16[128,4096]{1,0:T(8,128)(2,1)S(1)}, bf16[128,4096]{1,0:T(8,128)(2,1)}, u32[]{:S(2)}, u32[]{:S(2)}) collective-permute-start(bf16[128,4096]{1,0:T(8,128)(2,1)S(1)} %get-tuple-element.25), channel_id=1, source_target_pairs={{0,112},{4,116},{8,120},{12,124},{1,113},{5,117},{9,121},{13,125},... | collective-permute-start | bytes 3145736 | tf_op jit(solution)/shard_map/ppermute | solution.py:14
  178.8 0.7 fusion.26
  183.8 15.1 %collective-permute-done.4 = bf16[128,4096]{1,0:T(8,128)(2,1)} collective-permute-done((bf16[128,4096]{1,0:T(8,128)(2,1)}, bf16[128,4096]{1,0:T(8,128)(2,1)}, u32[]{:S(2)}, u32[]{:S(2)}) %collective-permute-start.4) | collective-permute-done | bytes 1048608 | tf_op jit(solution)/shard_map/ppermute | solution.py:14
  198.9 11.4 %collective-permute-done.6 = bf16[128,4096]{1,0:T(8,128)(2,1)} collective-permute-done((bf16[128,4096]{1,0:T(8,128)(2,1)S(1)}, bf16[128,4096]{1,0:T(8,128)(2,1)}, u32[]{:S(2)}, u32[]{:S(2)}) %collective-permute-start.6) | collective-permute-done | bytes 1048608 | tf_op jit(solution)/shard_map/ppermute | solution.py:14
  210.3 5.8 %add_convert_fusion = bf16[128,4096]{1,0:T(8,128)(2,1)S(1)} fusion(bf16[128,4096]{1,0:T(8,128)(2,1)} %collective-permute-done.6, bf16[128,4096]{1,0:T(8,128)(2,1)} %collective-permute-done.5, bf16[128,4096]{1,0:T(8,128)(2,1)} %collective-permute-done.4, bf16[128,4096]{1,0:T(8,128)(2,1)} %collective-permute-done.3, ...), kind=kLoop, calls=%fused_computation.20 | loop fusion | flops 14680064 | bytes 10485792 | tf_op jit(solution)/shard_map/convert_element_type | solution.py:109
  216.2 21.2 %collective-permute-done.7 = bf16[128,4096]{1,0:T(8,128)(2,1)S(1)} collective-permute-done((bf16[128,4096]{1,0:T(8,128)(2,1)S(1)}, bf16[128,4096]{1,0:T(8,128)(2,1)S(1)}, u32[]{:S(2)}, u32[]{:S(2)}) %collective-permute-start.7) | collective-permute-done | bytes 1048608 | tf_op jit(solution)/shard_map/ppermute | solution.py:20
  237.4 1.0 copy.16
  (32 shorter events, 0.7 us)
Async XLA Ops:
  6.5 62.7 %copy-start = (bf16[1,4096,128]{2,1,0:T(8,128)(2,1)S(1)}, bf16[1,4096,128]{2,1,0:T(8,128)(2,1)}, u32[]{:S(2)}) copy-start(bf16[1,4096,128]{2,1,0:T(8,128)(2,1)} %param.10) | copy-start | bytes 3145732
  6.5 54.9 %all-gather.2.cloned.1.call-start = ((), (), s32[]{:S(2)}) async-start(), calls=%async_computation.1 | async-start | bytes 5242880 | tf_op jit(solution)/shard_map/all_gather | solution.py:70
  10.6 199.6 %reduce-scatter.2.cloned.1.call-start = ((), (), s32[]{:S(2)}) async-start(), calls=%async_computation.2 | async-start | bytes 5242880 | tf_op jit(solution)/shard_map/reduce_scatter | solution.py:102
  72.9 7.3 %copy-start.2 = (bf16[1,4096,128]{2,1,0:T(8,128)(2,1)S(1)}, bf16[1,4096,128]{2,1,0:T(8,128)(2,1)}, u32[]{:S(2)}) copy-start(bf16[1,4096,128]{2,1,0:T(8,128)(2,1)} %param.11) | copy-start | bytes 3145732
  80.2 9.9 %slice-start = ((s8[6291456]{0:T(1024)(128)(4,1)}), s8[4194304]{0:T(1024)(128)(4,1)S(1)}, s32[]{:S(2)}) async-start(s8[6291456]{0:T(1024)(128)(4,1)} %bitcast.82), calls=%async_computation.3 | async-start | bytes 8388608
  84.1 6.0 %slice-start.1 = ((s8[6291456]{0:T(1024)(128)(4,1)}), s8[2097152]{0:T(1024)(128)(4,1)S(1)}, s32[]{:S(2)}) async-start(s8[6291456]{0:T(1024)(128)(4,1)} %bitcast.82), calls=%async_computation.4 | async-start | bytes 4194304
  95.3 83.4 %copy-start.5 = (f32[32,8]{0,1:T(8,128)S(1)}, f32[32,8]{0,1:T(8,128)}, u32[]{:S(2)}) copy-start(f32[32,8]{0,1:T(8,128)} %param.13) | copy-start | bytes 3076
  95.3 114.9 %copy-start.1 = (bf16[1,128,4096]{2,1,0:T(8,128)(2,1)S(1)}, bf16[1,128,4096]{2,1,0:T(8,128)(2,1)}, u32[]{:S(2)}) copy-start(bf16[1,128,4096]{2,1,0:T(8,128)(2,1)} %param.7) | copy-start | bytes 3145732
  100.9 27.3 %collective-permute-start = (bf16[128,4096]{1,0:T(8,128)(2,1)S(1)}, bf16[128,4096]{1,0:T(8,128)(2,1)S(1)}, u32[]{:S(2)}, u32[]{:S(2)}) collective-permute-start(bf16[128,4096]{1,0:T(8,128)(2,1)S(1)} %get-tuple-element.13), channel_id=1, source_target_pairs={{0,16},{4,20},{8,24},{12,28},{16,32},{20,36},{24,40},{28,44},{32,4... | collective-permute-start | bytes 3145736 | tf_op jit(solution)/shard_map/ppermute | solution.py:14
  106.1 52.1 %collective-permute-start.1 = (bf16[128,4096]{1,0:T(8,128)(2,1)S(1)}, bf16[128,4096]{1,0:T(8,128)(2,1)S(1)}, u32[]{:S(2)}, u32[]{:S(2)}) collective-permute-start(bf16[128,4096]{1,0:T(8,128)(2,1)S(1)} %get-tuple-element.24), channel_id=1, source_target_pairs={{0,32},{4,36},{8,40},{12,44},{16,48},{20,52},{24,56},{28,60},{32,6... | collective-permute-start | bytes 3145736 | tf_op jit(solution)/shard_map/ppermute | solution.py:14
  109.5 74.3 %collective-permute-start.2 = (bf16[128,4096]{1,0:T(8,128)(2,1)}, bf16[128,4096]{1,0:T(8,128)(2,1)}, u32[]{:S(2)}, u32[]{:S(2)}) collective-permute-start(bf16[128,4096]{1,0:T(8,128)(2,1)} %get-tuple-element.22), channel_id=1, source_target_pairs={{0,48},{4,52},{8,56},{12,60},{16,64},{20,68},{24,72},{28,76},{32,8... | collective-permute-start | bytes 3145736 | tf_op jit(solution)/shard_map/ppermute | solution.py:14
  114.2 69.6 %collective-permute-start.3 = (bf16[128,4096]{1,0:T(8,128)(2,1)}, bf16[128,4096]{1,0:T(8,128)(2,1)}, u32[]{:S(2)}, u32[]{:S(2)}) collective-permute-start(bf16[128,4096]{1,0:T(8,128)(2,1)} %get-tuple-element.20), channel_id=1, source_target_pairs={{0,64},{4,68},{8,72},{12,76},{16,80},{20,84},{24,88},{28,92},{32,9... | collective-permute-start | bytes 3145736 | tf_op jit(solution)/shard_map/ppermute | solution.py:14
  117.0 81.9 %collective-permute-start.4 = (bf16[128,4096]{1,0:T(8,128)(2,1)}, bf16[128,4096]{1,0:T(8,128)(2,1)}, u32[]{:S(2)}, u32[]{:S(2)}) collective-permute-start(bf16[128,4096]{1,0:T(8,128)(2,1)} %get-tuple-element.14), channel_id=1, source_target_pairs={{0,80},{4,84},{8,88},{12,92},{16,96},{20,100},{24,104},{28,108},{3... | collective-permute-start | bytes 3145736 | tf_op jit(solution)/shard_map/ppermute | solution.py:14
  128.2 50.5 %copy-start.3 = (bf16[128,4096]{1,0:T(8,128)(2,1)}, bf16[128,4096]{1,0:T(8,128)(2,1)S(1)}, u32[]{:S(2)}) copy-start(bf16[128,4096]{1,0:T(8,128)(2,1)S(1)} %collective-permute-done) | copy-start | bytes 3145732
  128.2 70.7 %collective-permute-start.5 = (bf16[128,4096]{1,0:T(8,128)(2,1)}, bf16[128,4096]{1,0:T(8,128)(2,1)}, u32[]{:S(2)}, u32[]{:S(2)}) collective-permute-start(bf16[128,4096]{1,0:T(8,128)(2,1)} %get-tuple-element.26), channel_id=1, source_target_pairs={{0,96},{4,100},{8,104},{12,108},{16,112},{20,116},{24,120},{28,124... | collective-permute-start | bytes 3145736 | tf_op jit(solution)/shard_map/ppermute | solution.py:14
  158.2 20.5 %copy-start.4 = (bf16[128,4096]{1,0:T(8,128)(2,1)}, bf16[128,4096]{1,0:T(8,128)(2,1)S(1)}, u32[]{:S(2)}) copy-start(bf16[128,4096]{1,0:T(8,128)(2,1)S(1)} %collective-permute-done.1) | copy-start | bytes 3145732
  158.2 52.1 %collective-permute-start.6 = (bf16[128,4096]{1,0:T(8,128)(2,1)S(1)}, bf16[128,4096]{1,0:T(8,128)(2,1)}, u32[]{:S(2)}, u32[]{:S(2)}) collective-permute-start(bf16[128,4096]{1,0:T(8,128)(2,1)S(1)} %get-tuple-element.25), channel_id=1, source_target_pairs={{0,112},{4,116},{8,120},{12,124},{1,113},{5,117},{9,121},{13,125},... | collective-permute-start | bytes 3145736 | tf_op jit(solution)/shard_map/ppermute | solution.py:14
  216.1 21.3 %collective-permute-start.7 = (bf16[128,4096]{1,0:T(8,128)(2,1)S(1)}, bf16[128,4096]{1,0:T(8,128)(2,1)S(1)}, u32[]{:S(2)}, u32[]{:S(2)}) collective-permute-start(bf16[128,4096]{1,0:T(8,128)(2,1)S(1)} %add_convert_fusion), channel_id=1, source_target_pairs={{124,0},{0,4},{4,8},{8,12},{12,16},{16,20},{20,24},{24,28},{28,32}... | collective-permute-start | bytes 3145736 | tf_op jit(solution)/shard_map/ppermute | solution.py:20
Sparse Core Ops, SparseCore 0:
  10.8 50.6 all-gather.1
  95.5 47.1 reduce-scatter.1
where the time goes:
time: 246 us; the launch traced here: 245 us
  waiting for transfers between devices  107 us (43%)
  starting transfers between devices  68.9 us (28%)
  matrix products  33.5 us (14%)
  between operations  17.8 us (7%)
  other arithmetic  10.1 us (4%)
  local copies, waits for them, and re-layouts  7.55 us (3%)
    ppermute x7, starting transfers between devices, passed_along(): lax.ppermute(value, axis, [(source, source + steps) for source in range(f...  68.8 us
    all_gather x1, waiting for transfers between devices, on_device(): row_piece = lax.all_gather(normed, 'tensor', axis=0, tiled=True)  50.7 us
    ppermute x7, waiting for transfers between devices, passed_along(): lax.ppermute(value, axis, [(source, source + steps) for source in range(f...  35.4 us
    ppermute x1, waiting for transfers between devices, from_behind(): return lax.ppermute(block, axis, route)  21.2 us
    dot_general x1, matrix products, on_device(): jnp.dot(row_piece, query_local, preferred_element_type=jnp.float32)  7.47 us
    sub x1, matrix products, attend(): softmax_weights = jax.nn.softmax(scores, axis=-1).astype(jnp.bfloat16)  7.28 us
    dot_general x1, matrix products, attend(): jnp.einsum('gjts,sgd->tgjd', softmax_weights, value_rows, preferred_eleme...  5.99 us
    convert_element_type x1, other arithmetic, on_device(): (self_coefficient[0] * block_out.astype(jnp.float32) + history_sum).astyp...  5.81 us
  transfers between devices with their start and end apart: 10, of which 5 were waited for; matrix products, arithmetic and copies ran while one was open for 3% of the time, Pallas kernels for 0%

commit v1 on v0

--- a/solution.py
+++ b/solution.py
@@ -67,7 +67,21 @@
     query_local = query_weight[0]
     key_local = key_weight[0]
     value_local = value_weight[0]
-    row_piece = lax.all_gather(normed, "tensor", axis=0, tiled=True)
+
+    def cube_attach(unit, chip_axis):
+        pieces_in = [unit]
+        extent = jax.lax.axis_size(chip_axis)
+        for kk in range(extent - 1):
+            local_out = jax.lax.ppermute(
+                pieces_in[-1], chip_axis, [(num, (num + 1) % extent) for num in range(extent)]
+            )
+            pieces_in.append(local_out)
+        main = jnp.concatenate(pieces_in[::-1], 0)
+        response = jax.lax.axis_index(chip_axis)
+        parts_out = jnp.roll(main, (response + 1) * unit.shape[0], 0)
+        return parts_out
+
+    row_piece = cube_attach(normed, "tensor")
     query_part = jnp.dot(row_piece, query_local, preferred_element_type=jnp.float32).astype(
         jnp.bfloat16
     )

time: 246 us -> 278 us (1.13)
  waiting for transfers between devices: 107 us -> 130 us
  local copies, waits for them, and re-layouts: 7.55 us -> 18.1 us
    ppermute x0 -> x3, waiting for transfers between devices: none -> 73.8 us  [cube_attach(): jax.lax.ppermute(pieces_in[-1], chip_axis, [(num, (num + 1) % extent) for...]
    all_gather x1 -> x0, waiting for transfers between devices: 50.7 us -> none  [on_device(): row_piece = lax.all_gather(normed, 'tensor', axis=0, tiled=True)]
    unnamed x17 -> x27, local copies, waits for them, and re-layouts: 1.01 us -> 10.9 us
    ppermute x7, waiting for transfers between devices: 35.4 us -> 31.9 us  [passed_along(): lax.ppermute(value, axis, [(source, source + steps) for source in range(f...]
    ppermute x1, waiting for transfers between devices: 21.2 us -> 24.5 us  [from_behind(): return lax.ppermute(block, axis, route)]
    dot_general x1, matrix products: 7.47 us -> 4.28 us  [on_device(): jnp.dot(row_piece, query_local, preferred_element_type=jnp.float32)]
    ppermute x7, starting transfers between devices: 68.8 us -> 65.9 us  [passed_along(): lax.ppermute(value, axis, [(source, source + steps) for source in range(f...]
  transfers between devices with their start and end apart: 10 -> 12, of which waited for: 5 -> 7; matrix products, arithmetic and copies ran while one was open for 3% -> 2% of each run, Pallas kernels for 0% -> 0%
where the time goes in v1:
time: 278 us; the launch traced here: 277 us
  waiting for transfers between devices  130 us (47%)
  starting transfers between devices  68.1 us (24%)
  matrix products  32.6 us (12%)
  local copies, waits for them, and re-layouts  18.1 us (7%)
  between operations  18.1 us (7%)
  other arithmetic  9.88 us (4%)
    ppermute x3, waiting for transfers between devices, cube_attach(): jax.lax.ppermute(pieces_in[-1], chip_axis, [(num, (num + 1) % extent) for...  73.8 us
    ppermute x7, starting transfers between devices, passed_along(): lax.ppermute(value, axis, [(source, source + steps) for source in range(f...  65.9 us
    ppermute x7, waiting for transfers between devices, passed_along(): lax.ppermute(value, axis, [(source, source + steps) for source in range(f...  31.9 us
    ppermute x1, waiting for transfers between devices, from_behind(): return lax.ppermute(block, axis, route)  24.5 us
    unnamed x27, local copies, waits for them, and re-layouts  10.9 us
    dot_general x1, matrix products, on_device(): jnp.dot(row_piece, output_local, preferred_element_type=jnp.float32)  7.81 us
    sub x1, matrix products, attend(): softmax_weights = jax.nn.softmax(scores, axis=-1).astype(jnp.bfloat16)  7.28 us
    convert_element_type x1, other arithmetic, on_device(): (self_coefficient[0] * block_out.astype(jnp.float32) + history_sum).astyp...  6.01 us
  transfers between devices with their start and end apart: 12, of which 7 were waited for; matrix products, arithmetic and copies ran while one was open for 2% of the time, Pallas kernels for 0%

profile of v1, /device:TPU:0, one launch (start us, length us, event | category | flops | bytes accessed | tf_op | source)
XLA Modules:
  0.0 277.1 jit_solution(2245456512638156961)
XLA Ops:
  9.7 1.7 collective-permute-start
  11.4 24.4 %collective-permute-done = bf16[128,4096]{1,0:T(8,128)(2,1)S(1)} collective-permute-done((bf16[128,4096]{1,0:T(8,128)(2,1)S(1)}, bf16[128,4096]{1,0:T(8,128)(2,1)S(1)}, u32[]{:S(2)}, u32[]{:S(2)}) %collective-permute-start) | collective-permute-done | bytes 1048608 | tf_op jit(solution)/shard_map/ppermute | solution.py:75
  36.3 24.8 %collective-permute-done.1 = bf16[128,4096]{1,0:T(8,128)(2,1)} collective-permute-done((bf16[128,4096]{1,0:T(8,128)(2,1)S(1)}, bf16[128,4096]{1,0:T(8,128)(2,1)}, u32[]{:S(2)}, u32[]{:S(2)}) %collective-permute-start.1) | collective-permute-done | bytes 1048608 | tf_op jit(solution)/shard_map/ppermute | solution.py:75
  61.2 24.5 %collective-permute-done.2 = bf16[128,4096]{1,0:T(8,128)(2,1)} collective-permute-done((bf16[128,4096]{1,0:T(8,128)(2,1)}, bf16[128,4096]{1,0:T(8,128)(2,1)}, u32[]{:S(2)}, u32[]{:S(2)}) %collective-permute-start.2) | collective-permute-done | bytes 1048608 | tf_op jit(solution)/shard_map/ppermute | solution.py:75
  92.0 3.2 %copy-done.5 = bf16[1024,4096]{1,0:T(8,128)(2,1)} copy-done((bf16[1024,4096]{1,0:T(8,128)(2,1)}, bf16[1024,4096]{1,0:T(8,128)(2,1)S(1)}, u32[]{:S(2)}) %copy-start.5) | copy-done | bytes 8388632
  95.2 4.3 %fusion.24 = bf16[512,768]{1,0:T(8,128)(2,1)} fusion(bf16[1,4096,768]{2,1,0:T(8,128)(2,1)S(1)} %bitcast.82, bf16[1024,4096]{1,0:T(8,128)(2,1)S(1)} %constant_dynamic-update-slice_fusion, s32[]{:T(128)S(6)} %select_n.41), kind=kOutput, calls=%fused_computation.28 | convolution fusion | flops 3221618688 | bytes 11272196 | tf_op jit(solution)/shard_map/dot_general | solution.py:85
  101.0 3.8 %fusion.32 = bf16[512,128]{0,1:T(8,128)(2,1)S(1)} fusion(bf16[1024,4096]{1,0:T(8,128)(2,1)} %copy-done.5, s32[]{:T(128)S(6)} %select_n.41, bf16[1,4096,128]{2,1,0:T(8,128)(2,1)S(1)} %copy-done), kind=kOutput, calls=%fused_computation.30 | convolution fusion | flops 536936448 | bytes 5373956 | tf_op jit(solution)/shard_map/dot_general | solution.py:88
  104.8 3.7 %fusion.29 = bf16[512,128]{0,1:T(8,128)(2,1)S(1)} fusion(bf16[1024,4096]{1,0:T(8,128)(2,1)} %copy-done.5, s32[]{:T(128)S(6)} %select_n.41, bf16[1,4096,128]{2,1,0:T(8,128)(2,1)S(1)} %copy-done.7), kind=kOutput, calls=%fused_computation.29 | convolution fusion | flops 536936448 | bytes 5373956 | tf_op jit(solution)/shard_map/dot_general | solution.py:91
  108.5 7.3 %fusion.43 = (f32[2,6,512]{2,1,0:T(8,128)S(1)}, f32[2,6,512,512]{2,3,1,0:T(8,128)}) fusion(pred[512,512]{0,1:T(8,128)(4,1)S(1)} %iota_compare_fusion, bf16[512,2,64,1]{0,2,3,1:T(8,128)(2,1)S(1)} %bitcast.85, bf16[512,2,6,64]{0,3,2,1:T(8,128)(2,1)S(1)} %bitcast.80), kind=kOutput, calls=%fused_computation.58 | convolution fusion | flops 415236608 | bytes 13787136 | tf_op jit(solution)/shard_map/while/body/eval_jaxpr/sub | solution.py:41
  115.8 5.8 %fusion.23 = bf16[2,64,6,512]{3,1,2,0:T(8,128)(2,1)S(1)} fusion(bf16[512,2,64,1]{0,2,3,1:T(8,128)(2,1)S(1)} %bitcast.84, f32[2,6,512,512]{2,3,1,0:T(8,128)} %get-tuple-element.36, f32[2,6,512]{2,1,0:T(8,128)S(1)} %get-tuple-element.35), kind=kOutput, calls=%fused_computation.27 | convolution fusion | flops 409337856 | bytes 13524992 | tf_op jit(solution)/shard_map/while/body/eval_jaxpr/gjts,sgd->tgjd/dot_general | solution.py:42
  121.5 7.8 %fusion.10 = bf16[512,4096]{1,0:T(8,128)(2,1)} fusion(bf16[512,768]{0,1:T(8,128)(2,1)S(1)} %bitcast.83, bf16[1,768,4096]{2,1,0:T(8,128)(2,1)} %param.12), kind=kOutput, calls=%fused_computation.13 | convolution fusion | flops 3223322624 | bytes 11272192 | tf_op jit(solution)/shard_map/dot_general | solution.py:113
  129.4 5.1 %slice_bitcast_fusion.6 = (bf16[128,4096]{1,0:T(8,128)(2,1)S(1)}, bf16[128,4096]{1,0:T(8,128)(2,1)}, bf16[128,4096]{1,0:T(8,128)(2,1)}, bf16[128,4096]{1,0:T(8,1...) fusion(bf16[1,7,128,4096]{3,2,1,0:T(8,128)(2,1)} %param.8), kind=kLoop, calls=%fused_computation.39 | loop fusion | bytes 14680064 | tf_op jit(solution)/shard_map/squeeze | solution.py:58
  134.5 6.2 %collective-permute-start.3 = (bf16[128,4096]{1,0:T(8,128)(2,1)S(1)}, bf16[128,4096]{1,0:T(8,128)(2,1)S(1)}, u32[]{:S(2)}, u32[]{:S(2)}) collective-permute-start(bf16[128,4096]{1,0:T(8,128)(2,1)S(1)} %get-tuple-element.13), channel_id=1, source_target_pairs={{0,16},{4,20},{8,24},{12,28},{16,32},{20,36},{24,40},{28,44},{32,4... | collective-permute-start | bytes 3145736 | tf_op jit(solution)/shard_map/ppermute | solution.py:14
  140.7 3.5 %collective-permute-start.4 = (bf16[128,4096]{1,0:T(8,128)(2,1)S(1)}, bf16[128,4096]{1,0:T(8,128)(2,1)S(1)}, u32[]{:S(2)}, u32[]{:S(2)}) collective-permute-start(bf16[128,4096]{1,0:T(8,128)(2,1)S(1)} %get-tuple-element.24), channel_id=1, source_target_pairs={{0,32},{4,36},{8,40},{12,44},{16,48},{20,52},{24,56},{28,60},{32,6... | collective-permute-start | bytes 3145736 | tf_op jit(solution)/shard_map/ppermute | solution.py:14
  144.2 4.2 %collective-permute-start.5 = (bf16[128,4096]{1,0:T(8,128)(2,1)}, bf16[128,4096]{1,0:T(8,128)(2,1)}, u32[]{:S(2)}, u32[]{:S(2)}) collective-permute-start(bf16[128,4096]{1,0:T(8,128)(2,1)} %get-tuple-element.22), channel_id=1, source_target_pairs={{0,48},{4,52},{8,56},{12,60},{16,64},{20,68},{24,72},{28,76},{32,8... | collective-permute-start | bytes 3145736 | tf_op jit(solution)/shard_map/ppermute | solution.py:14
  148.4 3.5 %collective-permute-start.6 = (bf16[128,4096]{1,0:T(8,128)(2,1)}, bf16[128,4096]{1,0:T(8,128)(2,1)}, u32[]{:S(2)}, u32[]{:S(2)}) collective-permute-start(bf16[128,4096]{1,0:T(8,128)(2,1)} %get-tuple-element.20), channel_id=1, source_target_pairs={{0,64},{4,68},{8,72},{12,76},{16,80},{20,84},{24,88},{28,92},{32,9... | collective-permute-start | bytes 3145736 | tf_op jit(solution)/shard_map/ppermute | solution.py:14
  152.0 2.3 collective-permute-start.7
  154.3 6.2 %collective-permute-done.3 = bf16[128,4096]{1,0:T(8,128)(2,1)S(1)} collective-permute-done((bf16[128,4096]{1,0:T(8,128)(2,1)S(1)}, bf16[128,4096]{1,0:T(8,128)(2,1)S(1)}, u32[]{:S(2)}, u32[]{:S(2)}) %collective-permute-start.3) | collective-permute-done | bytes 1048608 | tf_op jit(solution)/shard_map/ppermute | solution.py:14
  160.5 28.5 %collective-permute-start.8 = (bf16[128,4096]{1,0:T(8,128)(2,1)S(1)}, bf16[128,4096]{1,0:T(8,128)(2,1)}, u32[]{:S(2)}, u32[]{:S(2)}) collective-permute-start(bf16[128,4096]{1,0:T(8,128)(2,1)S(1)} %get-tuple-element.26), channel_id=1, source_target_pairs={{0,96},{4,100},{8,104},{12,108},{16,112},{20,116},{24,120},{28,124... | collective-permute-start | bytes 3145736 | tf_op jit(solution)/shard_map/ppermute | solution.py:14
  190.0 17.7 %collective-permute-start.9 = (bf16[128,4096]{1,0:T(8,128)(2,1)S(1)}, bf16[128,4096]{1,0:T(8,128)(2,1)}, u32[]{:S(2)}, u32[]{:S(2)}) collective-permute-start(bf16[128,4096]{1,0:T(8,128)(2,1)S(1)} %get-tuple-element.25), channel_id=1, source_target_pairs={{0,112},{4,116},{8,120},{12,124},{1,113},{5,117},{9,121},{13,125},... | collective-permute-start | bytes 3145736 | tf_op jit(solution)/shard_map/ppermute | solution.py:14
  213.0 18.4 %collective-permute-done.7 = bf16[128,4096]{1,0:T(8,128)(2,1)} collective-permute-done((bf16[128,4096]{1,0:T(8,128)(2,1)}, bf16[128,4096]{1,0:T(8,128)(2,1)}, u32[]{:S(2)}, u32[]{:S(2)}) %collective-permute-start.7) | collective-permute-done | bytes 1048608 | tf_op jit(solution)/shard_map/ppermute | solution.py:14
  231.3 7.3 %collective-permute-done.9 = bf16[128,4096]{1,0:T(8,128)(2,1)} collective-permute-done((bf16[128,4096]{1,0:T(8,128)(2,1)S(1)}, bf16[128,4096]{1,0:T(8,128)(2,1)}, u32[]{:S(2)}, u32[]{:S(2)}) %collective-permute-start.9) | collective-permute-done | bytes 1048608 | tf_op jit(solution)/shard_map/ppermute | solution.py:14
  238.6 6.0 %add_convert_fusion = bf16[128,4096]{1,0:T(8,128)(2,1)S(1)} fusion(bf16[128,4096]{1,0:T(8,128)(2,1)} %collective-permute-done.9, bf16[128,4096]{1,0:T(8,128)(2,1)} %collective-permute-done.8, bf16[128,4096]{1,0:T(8,128)(2,1)} %collective-permute-done.7, bf16[128,4096]{1,0:T(8,128)(2,1)} %collective-permute-done.6, ...), kind=kLoop, calls=%fused_computation.25 | loop fusion | flops 14680064 | bytes 10485792 | tf_op jit(solution)/shard_map/convert_element_type | solution.py:123
  244.7 24.5 %collective-permute-done.10 = bf16[128,4096]{1,0:T(8,128)(2,1)S(1)} collective-permute-done((bf16[128,4096]{1,0:T(8,128)(2,1)S(1)}, bf16[128,4096]{1,0:T(8,128)(2,1)S(1)}, u32[]{:S(2)}, u32[]{:S(2)}) %collective-permute-start.10) | collective-permute-done | bytes 1048608 | tf_op jit(solution)/shard_map/ppermute | solution.py:20
  (47 shorter events, 14.2 us)
Async XLA Ops:
  6.5 94.4 %copy-start = (bf16[1,4096,128]{2,1,0:T(8,128)(2,1)S(1)}, bf16[1,4096,128]{2,1,0:T(8,128)(2,1)}, u32[]{:S(2)}) copy-start(bf16[1,4096,128]{2,1,0:T(8,128)(2,1)} %param.10) | copy-start | bytes 3145732
  6.5 82.1 %copy-start.2 = (bf16[1,128,4096]{2,1,0:T(8,128)(2,1)S(1)}, bf16[1,128,4096]{2,1,0:T(8,128)(2,1)}, u32[]{:S(2)}) copy-start(bf16[1,128,4096]{2,1,0:T(8,128)(2,1)} %param.7) | copy-start | bytes 3145732
  6.5 232.1 %reduce-scatter.2.cloned.1.call-start = ((), (), s32[]{:S(2)}) async-start(), calls=%async_computation.1 | async-start | bytes 5242880 | tf_op jit(solution)/shard_map/reduce_scatter | solution.py:116
  9.7 26.1 %collective-permute-start = (bf16[128,4096]{1,0:T(8,128)(2,1)S(1)}, bf16[128,4096]{1,0:T(8,128)(2,1)S(1)}, u32[]{:S(2)}, u32[]{:S(2)}) collective-permute-start(bf16[128,4096]{1,0:T(8,128)(2,1)S(1)} %fusion.19), channel_id=1, source_target_pairs={{0,1},{1,2},{2,3},{3,0},{4,5},{5,6},{6,7},{7,4},{8,9},{9,10},{10,1... | collective-permute-start | bytes 3145736 | tf_op jit(solution)/shard_map/ppermute | solution.py:75
  35.8 25.3 %collective-permute-start.1 = (bf16[128,4096]{1,0:T(8,128)(2,1)S(1)}, bf16[128,4096]{1,0:T(8,128)(2,1)}, u32[]{:S(2)}, u32[]{:S(2)}) collective-permute-start(bf16[128,4096]{1,0:T(8,128)(2,1)S(1)} %collective-permute-done), channel_id=1, source_target_pairs={{0,1},{1,2},{2,3},{3,0},{4,5},{5,6},{6,7},{7,4},{8,9},{9,10},{10,1... | collective-permute-start | bytes 3145736 | tf_op jit(solution)/shard_map/ppermute | solution.py:75
  61.1 24.6 %collective-permute-start.2 = (bf16[128,4096]{1,0:T(8,128)(2,1)}, bf16[128,4096]{1,0:T(8,128)(2,1)}, u32[]{:S(2)}, u32[]{:S(2)}) collective-permute-start(bf16[128,4096]{1,0:T(8,128)(2,1)} %collective-permute-done.1), channel_id=1, source_target_pairs={{0,1},{1,2},{2,3},{3,0},{4,5},{5,6},{6,7},{7,4},{8,9},{9,10},{10,1... | collective-permute-start | bytes 3145736 | tf_op jit(solution)/shard_map/ppermute | solution.py:75
  87.0 8.2 %slice-start = ((s8[6291456]{0:T(1024)(128)(4,1)}), s8[4194304]{0:T(1024)(128)(4,1)S(1)}, s32[]{:S(2)}) async-start(s8[6291456]{0:T(1024)(128)(4,1)} %bitcast.81), calls=%async_computation.2 | async-start | bytes 8388608
  88.9 6.4 %slice-start.1 = ((s8[6291456]{0:T(1024)(128)(4,1)}), s8[2097152]{0:T(1024)(128)(4,1)S(1)}, s32[]{:S(2)}) async-start(s8[6291456]{0:T(1024)(128)(4,1)} %bitcast.81), calls=%async_computation.3 | async-start | bytes 4194304
  92.0 3.2 %copy-start.5 = (bf16[1024,4096]{1,0:T(8,128)(2,1)}, bf16[1024,4096]{1,0:T(8,128)(2,1)S(1)}, u32[]{:S(2)}) copy-start(bf16[1024,4096]{1,0:T(8,128)(2,1)S(1)} %constant_dynamic-update-slice_fusion) | copy-start | bytes 25165828
  100.9 3.8 %copy-start.7 = (bf16[1,4096,128]{2,1,0:T(8,128)(2,1)S(1)}, bf16[1,4096,128]{2,1,0:T(8,128)(2,1)}, u32[]{:S(2)}) copy-start(bf16[1,4096,128]{2,1,0:T(8,128)(2,1)} %param.11) | copy-start | bytes 3145732
  129.4 78.3 %copy-start.6 = (f32[32,8]{0,1:T(8,128)S(1)}, f32[32,8]{0,1:T(8,128)}, u32[]{:S(2)}) copy-start(f32[32,8]{0,1:T(8,128)} %param.13) | copy-start | bytes 3076
  134.5 26.0 %collective-permute-start.3 = (bf16[128,4096]{1,0:T(8,128)(2,1)S(1)}, bf16[128,4096]{1,0:T(8,128)(2,1)S(1)}, u32[]{:S(2)}, u32[]{:S(2)}) collective-permute-start(bf16[128,4096]{1,0:T(8,128)(2,1)S(1)} %get-tuple-element.13), channel_id=1, source_target_pairs={{0,16},{4,20},{8,24},{12,28},{16,32},{20,36},{24,40},{28,44},{32,4... | collective-permute-start | bytes 3145736 | tf_op jit(solution)/shard_map/ppermute | solution.py:14
  140.7 48.2 %collective-permute-start.4 = (bf16[128,4096]{1,0:T(8,128)(2,1)S(1)}, bf16[128,4096]{1,0:T(8,128)(2,1)S(1)}, u32[]{:S(2)}, u32[]{:S(2)}) collective-permute-start(bf16[128,4096]{1,0:T(8,128)(2,1)S(1)} %get-tuple-element.24), channel_id=1, source_target_pairs={{0,32},{4,36},{8,40},{12,44},{16,48},{20,52},{24,56},{28,60},{32,6... | collective-permute-start | bytes 3145736 | tf_op jit(solution)/shard_map/ppermute | solution.py:14
  144.2 68.7 %collective-permute-start.5 = (bf16[128,4096]{1,0:T(8,128)(2,1)}, bf16[128,4096]{1,0:T(8,128)(2,1)}, u32[]{:S(2)}, u32[]{:S(2)}) collective-permute-start(bf16[128,4096]{1,0:T(8,128)(2,1)} %get-tuple-element.22), channel_id=1, source_target_pairs={{0,48},{4,52},{8,56},{12,60},{16,64},{20,68},{24,72},{28,76},{32,8... | collective-permute-start | bytes 3145736 | tf_op jit(solution)/shard_map/ppermute | solution.py:14
  148.4 64.5 %collective-permute-start.6 = (bf16[128,4096]{1,0:T(8,128)(2,1)}, bf16[128,4096]{1,0:T(8,128)(2,1)}, u32[]{:S(2)}, u32[]{:S(2)}) collective-permute-start(bf16[128,4096]{1,0:T(8,128)(2,1)} %get-tuple-element.20), channel_id=1, source_target_pairs={{0,64},{4,68},{8,72},{12,76},{16,80},{20,84},{24,88},{28,92},{32,9... | collective-permute-start | bytes 3145736 | tf_op jit(solution)/shard_map/ppermute | solution.py:14
  152.0 79.4 %collective-permute-start.7 = (bf16[128,4096]{1,0:T(8,128)(2,1)}, bf16[128,4096]{1,0:T(8,128)(2,1)}, u32[]{:S(2)}, u32[]{:S(2)}) collective-permute-start(bf16[128,4096]{1,0:T(8,128)(2,1)} %get-tuple-element.14), channel_id=1, source_target_pairs={{0,80},{4,84},{8,88},{12,92},{16,96},{20,100},{24,104},{28,108},{3... | collective-permute-start | bytes 3145736 | tf_op jit(solution)/shard_map/ppermute | solution.py:14
  160.5 28.5 %copy-start.3 = (bf16[128,4096]{1,0:T(8,128)(2,1)}, bf16[128,4096]{1,0:T(8,128)(2,1)S(1)}, u32[]{:S(2)}) copy-start(bf16[128,4096]{1,0:T(8,128)(2,1)S(1)} %collective-permute-done.3) | copy-start | bytes 3145732
  160.5 70.8 %collective-permute-start.8 = (bf16[128,4096]{1,0:T(8,128)(2,1)S(1)}, bf16[128,4096]{1,0:T(8,128)(2,1)}, u32[]{:S(2)}, u32[]{:S(2)}) collective-permute-start(bf16[128,4096]{1,0:T(8,128)(2,1)S(1)} %get-tuple-element.26), channel_id=1, source_target_pairs={{0,96},{4,100},{8,104},{12,108},{16,112},{20,116},{24,120},{28,124... | collective-permute-start | bytes 3145736 | tf_op jit(solution)/shard_map/ppermute | solution.py:14
  189.0 1.0 copy-start.4
  190.0 48.6 %collective-permute-start.9 = (bf16[128,4096]{1,0:T(8,128)(2,1)S(1)}, bf16[128,4096]{1,0:T(8,128)(2,1)}, u32[]{:S(2)}, u32[]{:S(2)}) collective-permute-start(bf16[128,4096]{1,0:T(8,128)(2,1)S(1)} %get-tuple-element.25), channel_id=1, source_target_pairs={{0,112},{4,116},{8,120},{12,124},{1,113},{5,117},{9,121},{13,125},... | collective-permute-start | bytes 3145736 | tf_op jit(solution)/shard_map/ppermute | solution.py:14
  238.6 31.6 %copy-start.1 = (bf16[1,4096,128]{2,1,0:T(8,128)(2,1)S(1)}, bf16[1,4096,128]{2,1,0:T(8,128)(2,1)}, u32[]{:S(2)}) copy-start(bf16[1,4096,128]{2,1,0:T(8,128)(2,1)} %param.10) | copy-start | bytes 3145732
  244.6 24.6 %collective-permute-start.10 = (bf16[128,4096]{1,0:T(8,128)(2,1)S(1)}, bf16[128,4096]{1,0:T(8,128)(2,1)S(1)}, u32[]{:S(2)}, u32[]{:S(2)}) collective-permute-start(bf16[128,4096]{1,0:T(8,128)(2,1)S(1)} %add_convert_fusion), channel_id=1, source_target_pairs={{124,0},{0,4},{4,8},{8,12},{12,16},{16,20},{20,24},{24,28},{28,32}... | collective-permute-start | bytes 3145736 | tf_op jit(solution)/shard_map/ppermute | solution.py:20
Sparse Core Ops, SparseCore 0:
  129.5 47.0 reduce-scatter.1
